TPU v7x, 32 devices: a whole 2x2x4 slice. The times are simulated.
32 devices in a mesh: bank: 4 (over z), zero: 8 (over y, x, core).
Axes of the slice: x: 2, y: 2, z: 4, core: 2. Of those that a mesh axis runs over, the one named last changes fastest.
Arguments:
- w_gate: float32 [128, 2048, 768], P('bank', 'zero'), may hold values from -0.1875 to 0.1875
- w_up: float32 [128, 2048, 768], P('bank', 'zero'), may hold values from -0.1875 to 0.1875
- router_weight: float32 [2048, 128], P('zero', 'bank'), may hold values from -0.125 to 0.125
- router_gain: float32 [2048], P('zero'), may hold values from 0.25 to 1.75
Outputs:
- serve_gate: bfloat16 [128, 2048, 768], P('bank', None, 'zero')
- serve_up: bfloat16 [128, 2048, 768], P('bank', None, 'zero')
- scale_gate: float32 [128, 768], P('bank', 'zero')
- scale_up: float32 [128, 768], P('bank', 'zero')
- serve_router: bfloat16 [2048, 128], replicated
All inputs are finite; a program needn't handle non-finite values.
Results may differ from a plain program's by a relative error of at most 0.001.
Values may be sent and summed in bfloat16 or wider, within the bound.
A program may use at most 192 MiB of HBM per device.

v0:
```python
import jax
import jax.numpy as jnp
from jax import lax
from jax.sharding import PartitionSpec as P


def shards(w_gate, w_up, router_weight, router_gain):
    total_gate, total_up = lax.psum(
        (jnp.sum(w_gate * w_gate, axis=1), jnp.sum(w_up * w_up, axis=1)), "zero"
    )
    scale_gate = jnp.sqrt(total_gate)
    scale_up = jnp.sqrt(total_up)
    narrow_gate, narrow_up = (
        (w_gate / jnp.expand_dims(scale_gate, 1)).astype(jnp.bfloat16),
        (w_up / jnp.expand_dims(scale_up, 1)).astype(jnp.bfloat16),
    )
    serve_gate, serve_up = (
        lax.all_to_all(narrow_gate, "zero", split_axis=2, concat_axis=1, tiled=True),
        lax.all_to_all(narrow_up, "zero", split_axis=2, concat_axis=1, tiled=True),
    )
    scale_gate = lax.dynamic_slice_in_dim(
        scale_gate, lax.axis_index("zero") * serve_gate.shape[2], serve_gate.shape[2], axis=1
    )
    scale_up = lax.dynamic_slice_in_dim(
        scale_up, lax.axis_index("zero") * serve_up.shape[2], serve_up.shape[2], axis=1
    )
    part_router = (router_weight * router_gain[:, None]).astype(jnp.bfloat16)
    row_router = lax.all_gather(part_router, "zero", axis=0, tiled=True)
    serve_router = lax.all_gather(row_router, "bank", axis=1, tiled=True)
    return (serve_gate, serve_up, scale_gate, scale_up, serve_router)


def solution(mesh):
    placed = (P("bank", "zero", None), P("bank", "zero", None), P("zero", "bank"), P("zero"))
    return jax.shard_map(
        shards,
        mesh=mesh,
        in_specs=placed,
        out_specs=(
            P("bank", None, "zero"),
            P("bank", None, "zero"),
            P("bank", "zero"),
            P("bank", "zero"),
            P(),
        ),
        check_vma=False,
    )
```

profile of v0, /device:TPU:0, one launch (start us, length us, event | category | flops | bytes accessed | tf_op | source)
XLA Modules:
  0.0 481.0 jit_solution(10650282860068963028)
XLA Ops:
  7.2 0.0 all-reduce.3.cloned.1.call-start
  7.2 17.3 %multiply_reduce_fusion = (f32[32,768]{1,0:T(8,128)}, f32[32,768]{1,0:T(8,128)}) fusion(f32[32,256,768]{2,1,0:T(8,128)} %param.5, f32[32,256,768]{2,1,0:T(8,128)} %param.4), kind=kLoop, calls=%fused_computation.1 | loop fusion | flops 25116672 | bytes 50528256 | tf_op jit(solution)/shard_map/reduce_sum | solution.py:9
  24.5 0.0 all-reduce.3.cloned.1.call-update
  24.5 25.1 %copy.25 = f32[32,256,768]{1,0,2:T(8,128)} copy(f32[32,256,768]{2,1,0:T(8,128)} %param.5) | data formatting | bytes 50331648 | tf_op args[1]
  49.6 31.5 %all-reduce.3.cloned.1.call-done = (f32[32,768]{1,0:T(8,128)}, f32[32,768]{1,0:T(8,128)}) async-done(((f32[32,768]{1,0:T(8,128)}, f32[32,768]{1,0:T(8,128)}), (f32[32,768]{1,0:T(8,128)}, f32[32,768]{1,0:T(8,128)})) %all-reduce.3.cloned.1.call-update) | async-done | bytes 196624 | tf_op jit(solution)/shard_map/psum | solution.py:8
  81.1 0.9 sqrt.7
  82.1 0.2 copy.24
  82.2 14.1 %divide_convert_fusion = bf16[32,256,768]{1,0,2:T(8,128)(2,1)} fusion(f32[32,256,768]{1,0,2:T(8,128)} %copy.25, f32[32,768]{0,1:T(8,128)S(1)} %copy.24), kind=kLoop, calls=%fused_computation | loop fusion | flops 12582912 | bytes 37847040 | tf_op jit(solution)/shard_map/convert_element_type | solution.py:15
  96.4 5.4 %all-to-all-start.1 = ((bf16[32,256,768]{1,0,2:T(8,128)(2,1)}), bf16[32,256,768]{1,0,2:T(8,128)(2,1)}, u32[]{:S(2)}, u32[]{:S(2)}) async-start(bf16[32,256,768]{1,0,2:T(8,128)(2,1)} %divide_convert_fusion), calls=%async_computation.1 | async-start | bytes 25165824 | tf_op jit(solution)/shard_map/all_to_all | solution.py:19
  101.8 0.0 copy-start
  101.8 25.1 %copy.21 = f32[32,256,768]{1,0,2:T(8,128)} copy(f32[32,256,768]{2,1,0:T(8,128)} %param.4) | data formatting | bytes 50331648 | tf_op args[0]
  126.9 0.0 copy-done
  126.9 0.2 copy.20
  127.1 0.0 copy-start.1
  127.1 0.0 copy-start.2
  127.1 14.1 %divide_convert_fusion.1 = bf16[32,256,768]{1,0,2:T(8,128)(2,1)} fusion(f32[32,256,768]{1,0,2:T(8,128)} %copy.21, f32[32,768]{0,1:T(8,128)S(1)} %copy.20), kind=kLoop, calls=%fused_computation.2 | loop fusion | flops 12582912 | bytes 37847040 | tf_op jit(solution)/shard_map/convert_element_type | solution.py:14
  141.3 99.5 %all-to-all-done.1 = bf16[32,256,768]{1,0,2:T(8,128)(2,1)} async-done(((bf16[32,256,768]{1,0,2:T(8,128)(2,1)}), bf16[32,256,768]{1,0,2:T(8,128)(2,1)}, u32[]{:S(2)}, u32[]{:S(2)}) %all-to-all-start.1) | async-done | bytes 12582944 | tf_op jit(solution)/shard_map/all_to_all | solution.py:19
  240.8 5.4 %all-to-all-start = ((bf16[32,256,768]{1,0,2:T(8,128)(2,1)}), bf16[32,256,768]{1,0,2:T(8,128)(2,1)}, u32[]{:S(2)}, u32[]{:S(2)}) async-start(bf16[32,256,768]{1,0,2:T(8,128)(2,1)} %divide_convert_fusion.1), calls=%async_computation | async-start | bytes 25165824 | tf_op jit(solution)/shard_map/all_to_all | solution.py:18
  246.1 0.0 copy-done.1
  246.1 0.0 copy-done.2
  246.2 142.4 %all_gather.6 = bf16[2048,32]{0,1:T(8,128)(2,1)S(1)} all-gather(bf16[256,32]{0,1:T(8,128)(2,1)S(1)} %multiply_convert_fusion), channel_id=1, replica_groups=mesh['bank'=4,'zero'=8] {'zero'}, dimensions={0}, use_global_device_ids=true | all-gather | bytes 147456 | tf_op jit(solution)/shard_map/all_gather | solution.py:28
  388.6 16.1 %all_gather.7 = bf16[2048,128]{0,1:T(8,128)(2,1)S(1)} all-gather(bf16[2048,32]{0,1:T(8,128)(2,1)S(1)} %all_gather.6), channel_id=1, replica_groups=mesh['bank'=4,'zero'=8] {'bank'}, dimensions={1}, use_global_device_ids=true | all-gather | bytes 655360 | tf_op jit(solution)/shard_map/all_gather | solution.py:29
  404.6 1.0 copy.28
  405.6 0.7 constant_dynamic-slice_fusion
  406.3 0.7 constant_dynamic-slice_fusion.1
  407.0 14.1 %copy.27 = bf16[32,8,256,96]{2,1,3,0:T(8,128)(2,1)} copy(bf16[32,8,256,96]{2,0,3,1:T(8,128)(2,1)} %bitcast.5) | data formatting | bytes 25165824 | tf_op jit(solution)/shard_map/all_to_all | solution.py:19
  421.1 19.5 %all_to_all.33 = bf16[32,2048,96]{1,2,0:T(8,128)(2,1)} reshape(bf16[32,8,256,96]{2,1,3,0:T(8,128)(2,1)} %copy.27) | data formatting | bytes 25165824 | tf_op jit(solution)/shard_map/all_to_all | solution.py:19
  440.6 0.0 all-to-all-done
  440.6 14.1 %copy.23 = bf16[32,8,256,96]{2,1,3,0:T(8,128)(2,1)} copy(bf16[32,8,256,96]{2,0,3,1:T(8,128)(2,1)} %bitcast.2) | data formatting | bytes 25165824 | tf_op jit(solution)/shard_map/all_to_all | solution.py:18
  454.7 19.5 %all_to_all.29 = bf16[32,2048,96]{1,2,0:T(8,128)(2,1)} reshape(bf16[32,8,256,96]{2,1,3,0:T(8,128)(2,1)} %copy.23) | data formatting | bytes 25165824 | tf_op jit(solution)/shard_map/all_to_all | solution.py:18
  (2 shorter events, 0.0 us)
Async XLA Ops:
  7.2 74.0 %all-reduce.3.cloned.1.call-start = ((), (), s32[]{:S(2)}) async-start(), calls=%async_computation.2 | async-start | bytes 393216 | tf_op jit(solution)/shard_map/psum | solution.py:8
  96.4 144.4 %all-to-all-start.1 = ((bf16[32,256,768]{1,0,2:T(8,128)(2,1)}), bf16[32,256,768]{1,0,2:T(8,128)(2,1)}, u32[]{:S(2)}, u32[]{:S(2)}) async-start(bf16[32,256,768]{1,0,2:T(8,128)(2,1)} %divide_convert_fusion), calls=%async_computation.1 | async-start | bytes 25165824 | tf_op jit(solution)/shard_map/all_to_all | solution.py:19
  101.8 25.1 %copy-start = (f32[32,768]{1,0:T(8,128)S(1)}, f32[32,768]{1,0:T(8,128)}, u32[]{:S(2)}) copy-start(f32[32,768]{1,0:T(8,128)} %get-tuple-element.10) | copy-start | bytes 294916
  127.1 119.0 %copy-start.1 = (f32[256,32]{0,1:T(8,128)S(1)}, f32[256,32]{0,1:T(8,128)}, u32[]{:S(2)}) copy-start(f32[256,32]{0,1:T(8,128)} %param.6) | copy-start | bytes 98308
  127.1 119.0 %copy-start.2 = (f32[256]{0:T(256)S(1)}, f32[256]{0:T(256)}, u32[]{:S(2)}) copy-start(f32[256]{0:T(256)} %param.7) | copy-start | bytes 3076
  240.8 199.8 %all-to-all-start = ((bf16[32,256,768]{1,0,2:T(8,128)(2,1)}), bf16[32,256,768]{1,0,2:T(8,128)(2,1)}, u32[]{:S(2)}, u32[]{:S(2)}) async-start(bf16[32,256,768]{1,0,2:T(8,128)(2,1)} %divide_convert_fusion.1), calls=%async_computation | async-start | bytes 25165824 | tf_op jit(solution)/shard_map/all_to_all | solution.py:18
Sparse Core Ops, SparseCore 0:
  24.6 56.4 all-reduce.2
where the time goes:
time: 483 us; the launch traced here: 481 us
  blocking collectives  158 us (33%)
  waiting for transfers between devices  131 us (27%)
  local copies, waits for them, and re-layouts  121 us (25%)
  other arithmetic  45.5 us (9%)
  between operations  14.1 us (3%)
  starting transfers between devices  10.8 us (2%)
    all_gather x1, blocking collectives, shards(): row_router = lax.all_gather(part_router, 'zero', axis=0, tiled=True)  142 us
    all_to_all x1, waiting for transfers between devices, shards(): lax.all_to_all(narrow_up, 'zero', split_axis=2, concat_axis=1, tiled=True)  99.5 us
    unnamed x9, local copies, waits for them, and re-layouts  51.3 us
    all_to_all x2, local copies, waits for them, and re-layouts, shards(): lax.all_to_all(narrow_gate, 'zero', split_axis=2, concat_axis=1, tiled=True)  33.6 us
    all_to_all x2, local copies, waits for them, and re-layouts, shards(): lax.all_to_all(narrow_up, 'zero', split_axis=2, concat_axis=1, tiled=True)  33.6 us
    psum x1, waiting for transfers between devices, shards(): lax.psum((jnp.sum(w_gate * w_gate, axis=1), jnp.sum(w_up * w_up, axis=1))...  31.5 us
    reduce_sum x1, other arithmetic, shards(): jnp.sum(w_up * w_up, axis=1)  17.3 us
    all_gather x1, blocking collectives, shards(): serve_router = lax.all_gather(row_router, 'bank', axis=1, tiled=True)  16.1 us
  transfers between devices with their start and end apart: 3, of which 2 were waited for; matrix products, arithmetic and copies ran while one was open for 17% of the time, Pallas kernels for 0%

commit v1 on v0

--- a/solution.py
+++ b/solution.py
@@ -15,7 +15,12 @@
         (w_up / jnp.expand_dims(scale_up, 1)).astype(jnp.bfloat16),
     )
     serve_gate, serve_up = (
-        lax.all_to_all(narrow_gate, "zero", split_axis=2, concat_axis=1, tiled=True),
+        jnp.concatenate(
+            lax.all_to_all(
+                jnp.stack(jnp.split(narrow_gate, lax.axis_size("zero"), axis=2)), "zero", 0, 0
+            ),
+            axis=1,
+        ),
         lax.all_to_all(narrow_up, "zero", split_axis=2, concat_axis=1, tiled=True),
     )
     scale_gate = lax.dynamic_slice_in_dim(

time: 483 us -> 466 us (0.965)
  local copies, waits for them, and re-layouts: 121 us -> 108 us
    all_to_all x1, waiting for transfers between devices: 0.01 us -> 99.5 us  [shards(): lax.all_to_all(jnp.stack(jnp.split(narrow_gate, lax.axis_size('zero'), ax...]
    all_to_all x1, waiting for transfers between devices: 99.5 us -> 0.01 us  [shards(): lax.all_to_all(narrow_up, 'zero', split_axis=2, concat_axis=1, tiled=True)]
    all_to_all x2 -> x0, local copies, waits for them, and re-layouts: 33.6 us -> none  [shards(): lax.all_to_all(narrow_gate, 'zero', split_axis=2, concat_axis=1, tiled=True)]
    reshape x0 -> x1, local copies, waits for them, and re-layouts: none -> 10.9 us  [shards(): jnp.concatenate(lax.all_to_all(jnp.stack(jnp.split(narrow_gate, lax.axis_...]
    unnamed x9 -> x16, local copies, waits for them, and re-layouts: 51.3 us -> 59.8 us
where the time goes in v1:
time: 466 us; the launch traced here: 465 us
  blocking collectives  158 us (34%)
  waiting for transfers between devices  132 us (28%)
  local copies, waits for them, and re-layouts  108 us (23%)
  other arithmetic  41.7 us (9%)
  between operations  14.1 us (3%)
  starting transfers between devices  10.8 us (2%)
    all_gather x1, blocking collectives, shards(): row_router = lax.all_gather(part_router, 'zero', axis=0, tiled=True)  142 us
    all_to_all x1, waiting for transfers between devices, shards(): lax.all_to_all(jnp.stack(jnp.split(narrow_gate, lax.axis_size('zero'), ax...  99.5 us
    unnamed x16, local copies, waits for them, and re-layouts  59.8 us
    all_to_all x2, local copies, waits for them, and re-layouts, shards(): lax.all_to_all(narrow_up, 'zero', split_axis=2, concat_axis=1, tiled=True)  33.6 us
    psum x1, waiting for transfers between devices, shards(): lax.psum((jnp.sum(w_gate * w_gate, axis=1), jnp.sum(w_up * w_up, axis=1))...  32 us
    reduce_sum x1, other arithmetic, shards(): jnp.sum(w_up * w_up, axis=1)  17.3 us
    all_gather x1, blocking collectives, shards(): serve_router = lax.all_gather(row_router, 'bank', axis=1, tiled=True)  16.1 us
    convert_element_type x1, other arithmetic, shards(): (w_up / jnp.expand_dims(scale_up, 1)).astype(jnp.bfloat16)  14.1 us
  transfers between devices with their start and end apart: 3, of which 2 were waited for; matrix products, arithmetic and copies ran while one was open for 17% of the time, Pallas kernels for 0%

profile of v1, /device:TPU:0, one launch (start us, length us, event | category | flops | bytes accessed | tf_op | source)
XLA Modules:
  0.0 464.5 jit_solution(98903679744253797)
XLA Ops:
  7.2 0.0 all-reduce.3.cloned.1.call-start
  7.2 17.3 %multiply_reduce_fusion = (f32[32,768]{1,0:T(8,128)}, f32[32,768]{1,0:T(8,128)}) fusion(f32[32,256,768]{2,1,0:T(8,128)} %param.5, f32[32,256,768]{2,1,0:T(8,128)} %param.4), kind=kLoop, calls=%fused_computation.1 | loop fusion | flops 25116672 | bytes 50528256 | tf_op jit(solution)/shard_map/reduce_sum | solution.py:9
  24.5 0.0 all-reduce.3.cloned.1.call-update
  24.5 24.7 %copy.25 = f32[32,256,768]{1,2,0:T(8,128)} copy(f32[32,256,768]{2,1,0:T(8,128)} %param.4) | data formatting | bytes 50331648 | tf_op args[0]
  49.2 32.0 %all-reduce.3.cloned.1.call-done = (f32[32,768]{1,0:T(8,128)}, f32[32,768]{1,0:T(8,128)}) async-done(((f32[32,768]{1,0:T(8,128)}, f32[32,768]{1,0:T(8,128)}), (f32[32,768]{1,0:T(8,128)}, f32[32,768]{1,0:T(8,128)})) %all-reduce.3.cloned.1.call-update) | async-done | bytes 196624 | tf_op jit(solution)/shard_map/psum | solution.py:8
  81.1 0.9 sqrt.6
  82.1 10.3 %divide_convert_fusion.1 = bf16[32,256,768]{1,2,0:T(8,128)(2,1)S(1)} fusion(f32[32,256,768]{1,2,0:T(8,128)} %copy.25, f32[32,768]{1,0:T(8,128)S(1)} %sqrt.6), kind=kLoop, calls=%fused_computation.2 | loop fusion | flops 12582912 | bytes 37847040 | tf_op jit(solution)/shard_map/convert_element_type | solution.py:14
  92.3 1.3 fusion.7
  93.6 1.3 fusion.6
  94.9 1.3 fusion.5
  96.2 1.3 fusion.4
  97.5 1.3 fusion.3
  98.7 1.3 fusion.2
  100.0 1.3 fusion.1
  101.3 1.3 fusion
  102.6 5.4 %all-to-all-start = ((bf16[8,32,256,96]{2,3,1,0:T(8,128)(2,1)}), bf16[8,32,256,96]{2,3,1,0:T(8,128)(2,1)}, u32[]{:S(2)}, u32[]{:S(2)}) async-start(bf16[8,32,256,96]{2,3,1,0:T(8,128)(2,1)} %fusion), calls=%async_computation | async-start | bytes 25165824 | tf_op jit(solution)/shard_map/all_to_all | solution.py:19
  108.0 0.0 copy-start
  108.0 25.1 %copy.28 = f32[32,256,768]{1,0,2:T(8,128)} copy(f32[32,256,768]{2,1,0:T(8,128)} %param.5) | data formatting | bytes 50331648 | tf_op args[1]
  133.1 0.0 copy-done
  133.2 0.2 copy.27
  133.3 14.1 %divide_convert_fusion = bf16[32,256,768]{1,0,2:T(8,128)(2,1)} fusion(f32[32,256,768]{1,0,2:T(8,128)} %copy.28, f32[32,768]{0,1:T(8,128)S(1)} %copy.27), kind=kLoop, calls=%fused_computation | loop fusion | flops 12582912 | bytes 37847040 | tf_op jit(solution)/shard_map/convert_element_type | solution.py:15
  147.5 0.0 copy-start.1
  147.5 0.0 copy-start.2
  147.5 99.5 %all-to-all-done = bf16[8,32,256,96]{2,3,1,0:T(8,128)(2,1)} async-done(((bf16[8,32,256,96]{2,3,1,0:T(8,128)(2,1)}), bf16[8,32,256,96]{2,3,1,0:T(8,128)(2,1)}, u32[]{:S(2)}, u32[]{:S(2)}) %all-to-all-start) | async-done | bytes 12582944 | tf_op jit(solution)/shard_map/all_to_all | solution.py:19
  247.0 5.4 %all-to-all-start.1 = ((bf16[32,256,768]{1,0,2:T(8,128)(2,1)}), bf16[32,256,768]{1,0,2:T(8,128)(2,1)}, u32[]{:S(2)}, u32[]{:S(2)}) async-start(bf16[32,256,768]{1,0,2:T(8,128)(2,1)} %divide_convert_fusion), calls=%async_computation.1 | async-start | bytes 25165824 | tf_op jit(solution)/shard_map/all_to_all | solution.py:24
  252.3 0.0 copy-done.1
  252.4 0.0 copy-done.2
  252.4 142.4 %all_gather.6 = bf16[2048,32]{0,1:T(8,128)(2,1)S(1)} all-gather(bf16[256,32]{0,1:T(8,128)(2,1)S(1)} %multiply_convert_fusion), channel_id=1, replica_groups=mesh['bank'=4,'zero'=8] {'zero'}, dimensions={0}, use_global_device_ids=true | all-gather | bytes 147456 | tf_op jit(solution)/shard_map/all_gather | solution.py:33
  394.8 16.1 %all_gather.7 = bf16[2048,128]{0,1:T(8,128)(2,1)S(1)} all-gather(bf16[2048,32]{0,1:T(8,128)(2,1)S(1)} %all_gather.6), channel_id=1, replica_groups=mesh['bank'=4,'zero'=8] {'bank'}, dimensions={1}, use_global_device_ids=true | all-gather | bytes 655360 | tf_op jit(solution)/shard_map/all_gather | solution.py:34
  410.9 1.0 copy.31
  411.9 0.7 constant_dynamic-slice_fusion
  412.5 0.7 constant_dynamic-slice_fusion.1
  413.2 10.9 %copy.33 = bf16[8,32,12,8,256]{4,3,0,2,1:T(8,128)(2,1)} copy(bf16[8,32,12,8,256]{4,3,2,1,0:T(8,128)(2,1)} %bitcast.12) | data formatting | bytes 25165824 | tf_op jit(solution)/shard_map/reshape | solution.py:18
  424.1 0.0 all-to-all-done.1
  424.1 14.1 %copy.30 = bf16[32,8,256,96]{2,1,3,0:T(8,128)(2,1)} copy(bf16[32,8,256,96]{2,0,3,1:T(8,128)(2,1)} %bitcast.11) | data formatting | bytes 25165824 | tf_op jit(solution)/shard_map/all_to_all | solution.py:24
  438.2 19.5 %all_to_all.20 = bf16[32,2048,96]{1,2,0:T(8,128)(2,1)} reshape(bf16[32,8,256,96]{2,1,3,0:T(8,128)(2,1)} %copy.30) | data formatting | bytes 25165824 | tf_op jit(solution)/shard_map/all_to_all | solution.py:24
  (2 shorter events, 0.0 us)
Async XLA Ops:
  7.2 74.0 %all-reduce.3.cloned.1.call-start = ((), (), s32[]{:S(2)}) async-start(), calls=%async_computation.2 | async-start | bytes 393216 | tf_op jit(solution)/shard_map/psum | solution.py:8
  102.6 144.4 %all-to-all-start = ((bf16[8,32,256,96]{2,3,1,0:T(8,128)(2,1)}), bf16[8,32,256,96]{2,3,1,0:T(8,128)(2,1)}, u32[]{:S(2)}, u32[]{:S(2)}) async-start(bf16[8,32,256,96]{2,3,1,0:T(8,128)(2,1)} %fusion), calls=%async_computation | async-start | bytes 25165824 | tf_op jit(solution)/shard_map/all_to_all | solution.py:19
  108.0 25.1 %copy-start = (f32[32,768]{1,0:T(8,128)S(1)}, f32[32,768]{1,0:T(8,128)}, u32[]{:S(2)}) copy-start(f32[32,768]{1,0:T(8,128)} %get-tuple-element.16) | copy-start | bytes 294916
  147.5 104.9 %copy-start.1 = (f32[256,32]{0,1:T(8,128)S(1)}, f32[256,32]{0,1:T(8,128)}, u32[]{:S(2)}) copy-start(f32[256,32]{0,1:T(8,128)} %param.6) | copy-start | bytes 98308
  147.5 104.9 %copy-start.2 = (f32[256]{0:T(256)S(1)}, f32[256]{0:T(256)}, u32[]{:S(2)}) copy-start(f32[256]{0:T(256)} %param.7) | copy-start | bytes 3076
  247.0 177.1 %all-to-all-start.1 = ((bf16[32,256,768]{1,0,2:T(8,128)(2,1)}), bf16[32,256,768]{1,0,2:T(8,128)(2,1)}, u32[]{:S(2)}, u32[]{:S(2)}) async-start(bf16[32,256,768]{1,0,2:T(8,128)(2,1)} %divide_convert_fusion), calls=%async_computation.1 | async-start | bytes 25165824 | tf_op jit(solution)/shard_map/all_to_all | solution.py:24
Sparse Core Ops, SparseCore 0:
  24.6 56.4 all-reduce.2
